TPU v7x, 32 devices: a whole 2x2x4 slice. The times are simulated.
32 devices in a mesh: group: 2 (over x), frame: 4 (over y, core), row: 4 (over z).
Axes of the slice: x: 2, y: 2, z: 4, core: 2. Of those that a mesh axis runs over, the one named last changes fastest.
Arguments:
- latents: bfloat16 [48, 8, 64, 320], P(('group', 'frame'), 'row'), parts along dimension 0, may hold values from -8 to 8
- condition: bfloat16 [24, 8, 64, 320], P(('group', 'frame'), 'row'), parts along dimension 0, may hold values from -6 to 6
- key_frames: int32 [24], P('group'), parts along dimension 0, may hold values from -1 to 23, as said below
- propagate: int32 [48], P('group'), parts along dimension 0, may hold values from 0 to 11, as said below
- encoder_conv: bfloat16 [9, 320, 320], replicated, may hold values from -0.109375 to 0.109375
- zero_conv: bfloat16 [320, 320], replicated, may hold values from -0.3125 to 0.3125
- attention_gain: float32 [320], replicated, may hold values from 0.25 to 1.75
- query_weight: bfloat16 [320, 320], replicated, may hold values from -3 to 3
- key_weight: bfloat16 [320, 320], replicated, may hold values from -3 to 3
- value_weight: bfloat16 [320, 320], replicated, may hold values from -0.3125 to 0.3125
- output_weight: bfloat16 [320, 320], replicated, may hold values from -0.3125 to 0.3125
- conv_gain: float32 [320], replicated, may hold values from 0.25 to 1.75
- block_conv: bfloat16 [9, 320, 320], replicated, may hold values from -0.109375 to 0.109375
Outputs:
- updated: bfloat16 [48, 8, 64, 320], P(('group', 'frame'), 'row'), parts along dimension 0
There are 2 independent parts, one for each index of `group`. A program takes and returns all parts, laid end to end along the dimension named above; an argument that names none is the same for every part. Nothing has to cross between parts.
Inputs may be any that keep to these rules, and one draw needn't show every extreme that they name: `key_frames`: the 3 slots of index d of frame hold keyframes of frames d * 6 to (d + 1) * 6 - 1, all different, live slots first; of index d and the index half the frame axis away, one holds 3 live keyframes and the other 1. `propagate`: each frame names a live slot of its own index of frame or of an adjacent one (no wrap); a keyframe's own frame names its own slot.
All inputs are finite; a program needn't handle non-finite values.
Results may differ from a plain program's by a relative error of at most 0.014.
Values may be sent and summed in bfloat16 or wider, within the bound.
A program may use at most 64 MiB of HBM per device.

v0:
```python
import math

import jax
import jax.numpy as jnp
from jax import lax
from jax.sharding import PartitionSpec as P

HEADS = 8


def extended(shard, sides, width):
    for axis, dim in sides:
        size, length = (lax.axis_size(axis), shard.shape[dim])
        up = [(i, (i + 1) % size) for i in range(size - 1)]
        down = [(j, i) for i, j in up]
        last = lax.slice_in_dim(shard, length - width, length, axis=dim)
        initial = lax.slice_in_dim(shard, 0, width, axis=dim)
        before = lax.ppermute(last, axis, up)
        after = lax.ppermute(initial, axis, down)
        shard = jnp.concatenate([before, shard, after], axis=dim)
    return shard


def layer_norm(values_in, scale_gain):
    average = jnp.mean(values_in, axis=-1, keepdims=True)
    centered = values_in - average
    variance = jnp.mean(centered * centered, axis=-1, keepdims=True)
    return centered * lax.rsqrt(variance + 1e-05) * scale_gain


def positions(frame_total, channels):
    frame_pos = jnp.arange(frame_total, dtype=jnp.float32)[:, None]
    half_index = jnp.arange(channels // 2, dtype=jnp.float32)
    frequency = jnp.exp(half_index * (-2.0 * math.log(10000.0) / channels))
    angles = frame_pos * frequency
    return jnp.stack([jnp.sin(angles), jnp.cos(angles)], axis=-1).reshape(frame_total, channels)


def conv_taps(padded, weights):
    slab_count, padded_rows, col_count, channels = padded.shape
    row_count = padded_rows - 2
    widened = jnp.pad(padded, ((0, 0), (0, 0), (1, 1), (0, 0)))
    running = jnp.zeros((slab_count * row_count * col_count, weights.shape[2]), jnp.float32)
    for row_off in range(3):
        for col_off in range(3):
            window = widened[
                :, row_off : row_off + row_count, col_off : col_off + col_count, :
            ].reshape(-1, channels)
            running = running + jnp.dot(
                window, weights[3 * row_off + col_off], preferred_element_type=jnp.float32
            )
    return running.reshape(slab_count, row_count, col_count, -1)


def shards(
    latents,
    condition,
    key_frames,
    propagate,
    encoder_conv,
    zero_conv,
    attention_gain,
    query_weight,
    key_weight,
    value_weight,
    output_weight,
    conv_gain,
    block_conv,
):
    frames_dev = latents.shape[0]
    channels = latents.shape[3]
    slot_count = condition.shape[0]
    head_dim = channels // HEADS
    axis_len = lax.axis_size("frame")
    total_frames = frames_dev * axis_len
    total_slots = slot_count * axis_len
    padded = extended(condition, (("row", 1),), 1)
    features = jax.nn.silu(conv_taps(padded, encoder_conv)).astype(jnp.bfloat16)
    projected = jnp.dot(
        features.reshape(-1, channels), zero_conv, preferred_element_type=jnp.float32
    )
    keyres = projected.astype(jnp.bfloat16).reshape(condition.shape)
    encoding = positions(total_frames, channels)
    latents_pix = lax.all_to_all(latents, "frame", split_axis=2, concat_axis=0, tiled=True)
    residual_pix = lax.all_to_all(keyres, "frame", split_axis=2, concat_axis=0, tiled=True)
    all_frames = jnp.arange(total_frames, dtype=jnp.int32)
    onehot = (
        propagate[:, None] - 0 == jnp.arange(residual_pix.shape[0], dtype=jnp.int32)[None, :]
    ).astype(jnp.bfloat16)
    picked = jnp.dot(
        onehot, residual_pix.reshape(residual_pix.shape[0], -1), preferred_element_type=jnp.float32
    ).reshape(latents_pix.shape)
    source_frame = jnp.sum(
        jnp.where(
            propagate[:, None] == jnp.arange(total_slots, dtype=jnp.int32)[None, :],
            key_frames[None, :],
            0,
        ),
        axis=1,
    )
    reach = jnp.exp(-jnp.abs(all_frames - source_frame).astype(jnp.float32) / (2 * frames_dev))
    hidden_pix = (latents_pix.astype(jnp.float32) + reach[:, None, None, None] * picked).astype(
        jnp.bfloat16
    )
    frame_count, row_count, col_count, _ = hidden_pix.shape
    normed = (
        layer_norm(hidden_pix.astype(jnp.float32), attention_gain) + encoding[:, None, None, :]
    ).astype(jnp.bfloat16)
    flattened = normed.reshape(-1, channels)
    head_shape = (frame_count, row_count * col_count, HEADS, head_dim)
    query = (
        jnp.dot(flattened, query_weight, preferred_element_type=jnp.float32)
        .astype(jnp.bfloat16)
        .reshape(head_shape)
    )
    key_proj = (
        jnp.dot(flattened, key_weight, preferred_element_type=jnp.float32)
        .astype(jnp.bfloat16)
        .reshape(head_shape)
    )
    value_proj = (
        jnp.dot(flattened, value_weight, preferred_element_type=jnp.float32)
        .astype(jnp.bfloat16)
        .reshape(head_shape)
    )
    scores = jnp.einsum(
        "fphd,gphd->phfg", query, key_proj, preferred_element_type=jnp.float32
    ) / math.sqrt(head_dim)
    weights_soft = jax.nn.softmax(scores, axis=-1).astype(jnp.bfloat16)
    mixed_heads = (
        jnp.einsum("phfg,gphd->fphd", weights_soft, value_proj, preferred_element_type=jnp.float32)
        .astype(jnp.bfloat16)
        .reshape(-1, channels)
    )
    projected = jnp.dot(mixed_heads, output_weight, preferred_element_type=jnp.float32)
    attended_pix = (
        (hidden_pix.astype(jnp.float32).reshape(-1, channels) + projected)
        .astype(jnp.bfloat16)
        .reshape(hidden_pix.shape)
    )
    attended = lax.all_to_all(attended_pix, "frame", split_axis=0, concat_axis=2, tiled=True)
    activated = jax.nn.silu(layer_norm(attended.astype(jnp.float32), conv_gain)).astype(
        jnp.bfloat16
    )
    padded_rows = extended(activated, (("row", 1),), 1)
    convolved = conv_taps(padded_rows, block_conv)
    return (attended.astype(jnp.float32) + convolved).astype(jnp.bfloat16)


def solution(mesh):
    placed = (
        P(("group", "frame"), "row", None, None),
        P(("group", "frame"), "row", None, None),
        P("group"),
        P("group"),
        P(),
        P(),
        P(),
        P(),
        P(),
        P(),
        P(),
        P(),
        P(),
    )
    return jax.shard_map(
        shards,
        mesh=mesh,
        in_specs=placed,
        out_specs=P(("group", "frame"), "row", None, None),
        check_vma=False,
    )
```

profile of v0, /device:TPU:0, one launch (start us, length us, event | category | flops | bytes accessed | tf_op | source)
XLA Modules:
  0.0 119.1 jit_solution(18311225892279663839)
XLA Ops:
  0.0 1.1 fusion.84
  1.1 5.0 %collective-permute-start = (bf16[3,1,64,320]{3,2,1,0:T(8,128)(2,1)S(1)}, bf16[3,1,64,320]{3,2,1,0:T(8,128)(2,1)S(1)}, u32[]{:S(2)}, u32[]{:S(2)}) collective-permute-start(bf16[3,1,64,320]{3,2,1,0:T(8,128)(2,1)S(1)} %get-tuple-element.23), channel_id=1, source_target_pairs={{0,1},{1,2},{2,3},{4,5},{5,6},{6,7},{8,9},{9,10},{10,11},{12,13},{... | collective-permute-start | bytes 368648 | tf_op jit(solution)/shard_map/ppermute | solution.py:18
  6.1 1.3 %collective-permute-start.1 = (bf16[3,1,64,320]{3,2,1,0:T(8,128)(2,1)S(1)}, bf16[3,1,64,320]{3,2,1,0:T(8,128)(2,1)S(1)}, u32[]{:S(2)}, u32[]{:S(2)}) collective-permute-start(bf16[3,1,64,320]{3,2,1,0:T(8,128)(2,1)S(1)} %get-tuple-element.24), channel_id=1, source_target_pairs={{1,0},{2,1},{3,2},{5,4},{6,5},{7,6},{9,8},{10,9},{11,10},{13,12},{... | collective-permute-start | bytes 368648 | tf_op jit(solution)/shard_map/ppermute | solution.py:19
  7.4 2.3 %copy.87 = bf16[6,2,64,320]{3,0,1,2:T(8,128)(2,1)} copy(bf16[6,2,64,320]{3,2,1,0:T(8,128)(2,1)} %param.13) | data formatting | bytes 983040 | tf_op args[0]
  9.7 3.6 %collective-permute-done.1 = bf16[3,1,64,320]{3,2,1,0:T(8,128)(2,1)S(1)} collective-permute-done((bf16[3,1,64,320]{3,2,1,0:T(8,128)(2,1)S(1)}, bf16[3,1,64,320]{3,2,1,0:T(8,128)(2,1)S(1)}, u32[]{:S(2)}, u32[]{:S(2)}) %collective-permute-start.1) | collective-permute-done | bytes 122912 | tf_op jit(solution)/shard_map/ppermute | solution.py:19
  13.8 1.3 %copy-done.5 = bf16[9,320,320]{2,1,0:T(8,128)(2,1)S(1)} copy-done((bf16[9,320,320]{2,1,0:T(8,128)(2,1)S(1)}, bf16[9,320,320]{2,1,0:T(8,128)(2,1)}, u32[]{:S(2)}) %copy-start.5) | copy-done | bytes 1843224
  18.5 1.7 %convolution_convert_fusion.4 = bf16[384,320]{0,1:T(8,128)(2,1)S(1)} fusion(bf16[320,320]{1,0:T(8,128)(2,1)S(1)} %copy-done.11, f32[384,320]{0,1:T(8,128)S(1)} %fusion.40, f32[384,320]{0,1:T(8,128)S(1)} %convolution_add_fusion.9, bf16[384,320]{1,0:T(8,128)(2,1)S(1)} %bitcast.195, bf16[9,320,320]{2,1,0:T(8,128)(2,1)} %param.17), kind=kOutput, calls=%fused_computation.45 | convolution fusion | flops 158269440 | bytes 1925120 | tf_op jit(solution)/shard_map/dot_general | solution.py:79
  20.4 1.0 copy.91
  21.4 3.6 %all-to-all-start.1 = ((bf16[3,2,64,320]{3,1,0,2:T(2,128)(2,1)}), bf16[3,2,64,320]{3,1,0,2:T(2,128)(2,1)S(1)}, u32[]{:S(2)}, u32[]{:S(2)}) async-start(bf16[3,2,64,320]{3,1,0,2:T(2,128)(2,1)} %copy.91), calls=%async_computation.1 | async-start | bytes 589824 | tf_op jit(solution)/shard_map/all_to_all | solution.py:85
  25.1 6.2 %all-to-all-done.1 = bf16[3,2,64,320]{3,1,0,2:T(2,128)(2,1)S(1)} async-done(((bf16[3,2,64,320]{3,1,0,2:T(2,128)(2,1)}), bf16[3,2,64,320]{3,1,0,2:T(2,128)(2,1)S(1)}, u32[]{:S(2)}, u32[]{:S(2)}) %all-to-all-start.1) | async-done | bytes 245792 | tf_op jit(solution)/shard_map/all_to_all | solution.py:85
  31.3 3.7 %all-to-all-start = ((bf16[6,2,64,320]{3,0,1,2:T(8,128)(2,1)}), bf16[6,2,64,320]{3,0,1,2:T(8,128)(2,1)S(1)}, u32[]{:S(2)}, u32[]{:S(2)}) async-start(bf16[6,2,64,320]{3,0,1,2:T(8,128)(2,1)} %copy.87), calls=%async_computation | async-start | bytes 1572864 | tf_op jit(solution)/shard_map/all_to_all | solution.py:84
  36.1 10.3 %all-to-all-done = bf16[6,2,64,320]{3,0,1,2:T(8,128)(2,1)S(1)} async-done(((bf16[6,2,64,320]{3,0,1,2:T(8,128)(2,1)}), bf16[6,2,64,320]{3,0,1,2:T(8,128)(2,1)S(1)}, u32[]{:S(2)}, u32[]{:S(2)}) %all-to-all-start) | async-done | bytes 491552 | tf_op jit(solution)/shard_map/all_to_all | solution.py:84
  47.8 1.3 %copy.96 = f32[24,2,16,320]{3,2,1,0:T(8,128)} copy(f32[24,2,16,320]{3,0,2,1:T(8,128)S(1)} %get-tuple-element.28) | data formatting | bytes 1966080 | tf_op jit(solution)/shard_map/convert_element_type | solution.py:137
  50.3 1.4 %reshape.271 = bf16[24,32,8,40]{1,0,3,2:T(8,128)(2,1)S(1)} reshape(bf16[768,320]{0,1:T(8,128)(2,1)S(1)} %convolution_convert_fusion.2) | data formatting | bytes 983040 | tf_op jit(solution)/shard_map/reshape | solution.py:114
  51.7 3.9 %copy.103 = bf16[24,32,8,40]{3,0,2,1:T(8,128)(2,1)} copy(bf16[24,32,8,40]{1,0,3,2:T(8,128)(2,1)S(1)} %reshape.271) | data formatting | bytes 983040 | tf_op jit(solution)/shard_map/reshape | solution.py:114
  55.6 1.4 %convolution_convert_fusion.1 = bf16[768,320]{0,1:T(8,128)(2,1)S(1)} fusion(bf16[768,320]{1,0:T(8,128)(2,1)S(1)} %bitcast.167, bf16[320,320]{1,0:T(8,128)(2,1)} %param.21), kind=kOutput, calls=%fused_computation.33 | convolution fusion | flops 157532160 | bytes 1187840 | tf_op jit(solution)/shard_map/dot_general | solution.py:117
  57.0 1.4 %reshape.272 = bf16[24,32,8,40]{1,0,3,2:T(8,128)(2,1)S(1)} reshape(bf16[768,320]{0,1:T(8,128)(2,1)S(1)} %convolution_convert_fusion.1) | data formatting | bytes 983040 | tf_op jit(solution)/shard_map/reshape | solution.py:119
  58.4 3.9 %copy.104 = bf16[24,32,8,40]{3,0,2,1:T(8,128)(2,1)} copy(bf16[24,32,8,40]{1,0,3,2:T(8,128)(2,1)S(1)} %reshape.272) | data formatting | bytes 983040 | tf_op jit(solution)/shard_map/reshape | solution.py:119
  62.3 1.4 %convolution_convert_fusion.3 = bf16[768,320]{0,1:T(8,128)(2,1)S(1)} fusion(bf16[768,320]{1,0:T(8,128)(2,1)S(1)} %bitcast.168, bf16[320,320]{1,0:T(8,128)(2,1)} %param.22), kind=kOutput, calls=%fused_computation.35 | convolution fusion | flops 157532160 | bytes 1187840 | tf_op jit(solution)/shard_map/dot_general | solution.py:122
  63.8 1.4 %reshape.270 = bf16[24,32,8,40]{1,0,3,2:T(8,128)(2,1)S(1)} reshape(bf16[768,320]{0,1:T(8,128)(2,1)S(1)} %convolution_convert_fusion.3) | data formatting | bytes 983040 | tf_op jit(solution)/shard_map/reshape | solution.py:124
  65.2 3.9 %copy.105 = bf16[24,32,8,40]{3,0,2,1:T(8,128)(2,1)} copy(bf16[24,32,8,40]{1,0,3,2:T(8,128)(2,1)S(1)} %reshape.270) | data formatting | bytes 983040 | tf_op jit(solution)/shard_map/reshape | solution.py:124
  69.1 5.4 %fusion.86 = (f32[32,8,24]{2,1,0:T(8,128)S(1)}, f32[32,8,24,24]{2,3,1,0:T(8,128)}) fusion(bf16[24,32,8,40]{3,0,2,1:T(8,128)(2,1)} %copy.103, bf16[24,32,8,40]{3,0,2,1:T(8,128)(2,1)} %copy.104), kind=kOutput, calls=%fused_computation.133 | convolution fusion | flops 12238871 | bytes 1597440 | tf_op jit(solution)/shard_map/sub | solution.py:129
  74.5 2.9 %fusion.10 = bf16[24,32,8,40]{3,0,2,1:T(8,128)(2,1)S(1)} fusion(bf16[24,32,8,40]{3,0,2,1:T(8,128)(2,1)S(1)} %copy-done.6, f32[32,8,24,24]{2,3,1,0:T(8,128)} %get-tuple-element.30, f32[32,8,24]{2,1,0:T(8,128)S(1)} %get-tuple-element.29), kind=kOutput, calls=%fused_computation.16 | convolution fusion | flops 12337152 | bytes 1597440 | tf_op jit(solution)/shard_map/phfg,gphd->fphd/dot_general | solution.py:131
  77.8 2.0 %reshape.253 = bf16[768,320]{1,0:T(8,128)(2,1)} reshape(bf16[24,32,8,40]{3,2,1,0:T(8,128)(2,1)S(1)} %copy.107) | data formatting | bytes 983040 | tf_op jit(solution)/shard_map/reshape | solution.py:133
  81.7 11.9 %all_to_all.33 = bf16[24,2,16,320]{3,2,1,0:T(8,128)(2,1)S(1)} all-to-all(bf16[24,2,16,320]{3,2,1,0:T(8,128)(2,1)S(1)} %bitcast.180), channel_id=1, replica_groups=mesh['group'=2,'frame'=4,'row'=4] {'frame'}, dimensions={0} | all-to-all | bytes 983040 | tf_op jit(solution)/shard_map/all_to_all | solution.py:141
  95.1 3.5 %collective-permute-start.2 = (bf16[6,1,64,320]{3,2,1,0:T(8,128)(2,1)S(1)}, bf16[6,1,64,320]{3,2,1,0:T(8,128)(2,1)S(1)}, u32[]{:S(2)}, u32[]{:S(2)}) collective-permute-start(bf16[6,1,64,320]{3,2,1,0:T(8,128)(2,1)S(1)} %get-tuple-element.19), channel_id=1, source_target_pairs={{0,1},{1,2},{2,3},{4,5},{5,6},{6,7},{8,9},{9,10},{10,11},{12,13},{... | collective-permute-start | bytes 737288 | tf_op jit(solution)/shard_map/ppermute | solution.py:18
  98.6 1.3 %collective-permute-start.3 = (bf16[6,1,64,320]{3,2,1,0:T(8,128)(2,1)S(1)}, bf16[6,1,64,320]{3,2,1,0:T(8,128)(2,1)S(1)}, u32[]{:S(2)}, u32[]{:S(2)}) collective-permute-start(bf16[6,1,64,320]{3,2,1,0:T(8,128)(2,1)S(1)} %get-tuple-element.20), channel_id=1, source_target_pairs={{1,0},{2,1},{3,2},{5,4},{6,5},{7,6},{9,8},{10,9},{11,10},{13,12},{... | collective-permute-start | bytes 737288 | tf_op jit(solution)/shard_map/ppermute | solution.py:19
  100.3 4.4 %collective-permute-done.2 = bf16[6,1,64,320]{3,2,1,0:T(8,128)(2,1)S(1)} collective-permute-done((bf16[6,1,64,320]{3,2,1,0:T(8,128)(2,1)S(1)}, bf16[6,1,64,320]{3,2,1,0:T(8,128)(2,1)S(1)}, u32[]{:S(2)}, u32[]{:S(2)}) %collective-permute-start.2) | collective-permute-done | bytes 245792 | tf_op jit(solution)/shard_map/ppermute | solution.py:18
  104.7 4.1 %collective-permute-done.3 = bf16[6,1,64,320]{3,2,1,0:T(8,128)(2,1)S(1)} collective-permute-done((bf16[6,1,64,320]{3,2,1,0:T(8,128)(2,1)S(1)}, bf16[6,1,64,320]{3,2,1,0:T(8,128)(2,1)S(1)}, u32[]{:S(2)}, u32[]{:S(2)}) %collective-permute-start.3) | collective-permute-done | bytes 245792 | tf_op jit(solution)/shard_map/ppermute | solution.py:19
  115.1 1.4 %fusion.12 = f32[768,320]{0,1:T(8,128)} fusion(f32[768,320]{0,1:T(8,128)S(1)} %fusion.29, f32[768,320]{0,1:T(8,128)S(1)} %convolution_add_fusion.1, bf16[768,320]{1,0:T(8,128)(2,1)S(1)} %bitcast.183, bf16[9,320,320]{2,1,0:T(8,128)(2,1)S(1)} %copy-done.4), kind=kOutput, calls=%fused_computation.20 | convolution fusion | flops 157777920 | bytes 3784704 | tf_op jit(solution)/shard_map/dot_general | solution.py:49
  116.6 1.6 %copy.111 = f32[768,320]{1,0:T(8,128)S(1)} copy(f32[768,320]{0,1:T(8,128)} %fusion.12) | data formatting | bytes 1966080 | tf_op jit(solution)/shard_map/add | solution.py:49
  118.1 1.0 fusion.22
  (84 shorter events, 18.0 us)
Async XLA Ops:
  0.0 49.8 %copy-start = (bf16[320,320]{1,0:T(8,128)(2,1)S(1)}, bf16[320,320]{1,0:T(8,128)(2,1)}, u32[]{:S(2)}) copy-start(bf16[320,320]{1,0:T(8,128)(2,1)} %param.20) | copy-start | bytes 614404
  0.0 13.3 %copy-start.2 = (bf16[3,2,64,320]{3,2,1,0:T(8,128)(2,1)S(1)}, bf16[3,2,64,320]{3,2,1,0:T(8,128)(2,1)}, u32[]{:S(2)}) copy-start(bf16[3,2,64,320]{3,2,1,0:T(8,128)(2,1)} %param.14) | copy-start | bytes 737284
  1.1 8.6 %collective-permute-start = (bf16[3,1,64,320]{3,2,1,0:T(8,128)(2,1)S(1)}, bf16[3,1,64,320]{3,2,1,0:T(8,128)(2,1)S(1)}, u32[]{:S(2)}, u32[]{:S(2)}) collective-permute-start(bf16[3,1,64,320]{3,2,1,0:T(8,128)(2,1)S(1)} %get-tuple-element.23), channel_id=1, source_target_pairs={{0,1},{1,2},{2,3},{4,5},{5,6},{6,7},{8,9},{9,10},{10,11},{12,13},{... | collective-permute-start | bytes 368648 | tf_op jit(solution)/shard_map/ppermute | solution.py:18
  6.1 7.2 %collective-permute-start.1 = (bf16[3,1,64,320]{3,2,1,0:T(8,128)(2,1)S(1)}, bf16[3,1,64,320]{3,2,1,0:T(8,128)(2,1)S(1)}, u32[]{:S(2)}, u32[]{:S(2)}) collective-permute-start(bf16[3,1,64,320]{3,2,1,0:T(8,128)(2,1)S(1)} %get-tuple-element.24), channel_id=1, source_target_pairs={{1,0},{2,1},{3,2},{5,4},{6,5},{7,6},{9,8},{10,9},{11,10},{13,12},{... | collective-permute-start | bytes 368648 | tf_op jit(solution)/shard_map/ppermute | solution.py:19
  13.5 1.6 %copy-start.5 = (bf16[9,320,320]{2,1,0:T(8,128)(2,1)S(1)}, bf16[9,320,320]{2,1,0:T(8,128)(2,1)}, u32[]{:S(2)}) copy-start(bf16[9,320,320]{2,1,0:T(8,128)(2,1)} %param.17) | copy-start | bytes 5529604
  17.5 0.9 copy-start.11
  21.4 13.8 %copy-start.10 = (s32[24]{0:T(128)S(1)}, s32[24]{0:T(128)}, u32[]{:S(2)}) copy-start(s32[24]{0:T(128)} %param.16) | copy-start | bytes 292
  21.4 13.8 %copy-start.12 = (s32[12]{0:T(128)S(1)}, s32[12]{0:T(128)}, u32[]{:S(2)}) copy-start(s32[12]{0:T(128)} %param.15) | copy-start | bytes 148
  21.4 9.9 %all-to-all-start.1 = ((bf16[3,2,64,320]{3,1,0,2:T(2,128)(2,1)}), bf16[3,2,64,320]{3,1,0,2:T(2,128)(2,1)S(1)}, u32[]{:S(2)}, u32[]{:S(2)}) async-start(bf16[3,2,64,320]{3,1,0,2:T(2,128)(2,1)} %copy.91), calls=%async_computation.1 | async-start | bytes 589824 | tf_op jit(solution)/shard_map/all_to_all | solution.py:85
  31.3 15.1 %all-to-all-start = ((bf16[6,2,64,320]{3,0,1,2:T(8,128)(2,1)}), bf16[6,2,64,320]{3,0,1,2:T(8,128)(2,1)S(1)}, u32[]{:S(2)}, u32[]{:S(2)}) async-start(bf16[6,2,64,320]{3,0,1,2:T(8,128)(2,1)} %copy.87), calls=%async_computation | async-start | bytes 1572864 | tf_op jit(solution)/shard_map/all_to_all | solution.py:84
  47.8 1.7 %copy-start.9 = (f32[320]{0:T(512)S(1)}, f32[320]{0:T(512)}, u32[]{:S(2)}) copy-start(f32[320]{0:T(512)} %param.19) | copy-start | bytes 3844
  69.1 5.4 %copy-start.6 = (bf16[24,32,8,40]{3,0,2,1:T(8,128)(2,1)S(1)}, bf16[24,32,8,40]{3,0,2,1:T(8,128)(2,1)}, u32[]{:S(2)}) copy-start(bf16[24,32,8,40]{3,0,2,1:T(8,128)(2,1)} %copy.105) | copy-start | bytes 1474564
  77.8 2.0 %copy-start.1 = (f32[24,2,16,320]{3,2,1,0:T(8,128)S(1)}, f32[24,2,16,320]{3,2,1,0:T(8,128)}, u32[]{:S(2)}) copy-start(f32[24,2,16,320]{3,2,1,0:T(8,128)} %copy.96) | copy-start | bytes 2949124
  79.8 1.1 copy-start.3
  79.8 1.1 copy-start.7
  93.8 0.8 copy-start.8
  95.1 9.7 %collective-permute-start.2 = (bf16[6,1,64,320]{3,2,1,0:T(8,128)(2,1)S(1)}, bf16[6,1,64,320]{3,2,1,0:T(8,128)(2,1)S(1)}, u32[]{:S(2)}, u32[]{:S(2)}) collective-permute-start(bf16[6,1,64,320]{3,2,1,0:T(8,128)(2,1)S(1)} %get-tuple-element.19), channel_id=1, source_target_pairs={{0,1},{1,2},{2,3},{4,5},{5,6},{6,7},{8,9},{9,10},{10,11},{12,13},{... | collective-permute-start | bytes 737288 | tf_op jit(solution)/shard_map/ppermute | solution.py:18
  98.6 10.3 %collective-permute-start.3 = (bf16[6,1,64,320]{3,2,1,0:T(8,128)(2,1)S(1)}, bf16[6,1,64,320]{3,2,1,0:T(8,128)(2,1)S(1)}, u32[]{:S(2)}, u32[]{:S(2)}) collective-permute-start(bf16[6,1,64,320]{3,2,1,0:T(8,128)(2,1)S(1)} %get-tuple-element.20), channel_id=1, source_target_pairs={{1,0},{2,1},{3,2},{5,4},{6,5},{7,6},{9,8},{10,9},{11,10},{13,12},{... | collective-permute-start | bytes 737288 | tf_op jit(solution)/shard_map/ppermute | solution.py:19
  109.5 1.6 %copy-start.4 = (bf16[9,320,320]{2,1,0:T(8,128)(2,1)S(1)}, bf16[9,320,320]{2,1,0:T(8,128)(2,1)}, u32[]{:S(2)}) copy-start(bf16[9,320,320]{2,1,0:T(8,128)(2,1)} %param.25) | copy-start | bytes 5529604
where the time goes:
time: 120 us; the launch traced here: 119 us
  local copies, waits for them, and re-layouts  32.3 us (27%)
  waiting for transfers between devices  28.6 us (24%)
  matrix products  22.9 us (19%)
  starting transfers between devices  18.3 us (15%)
  blocking collectives  11.9 us (10%)
  other arithmetic  4.6 us (4%)
    all_to_all x1, blocking collectives, shards(): lax.all_to_all(attended_pix, 'frame', split_axis=0, concat_axis=2, tiled=...  11.9 us
    all_to_all x1, waiting for transfers between devices, shards(): lax.all_to_all(latents, 'frame', split_axis=2, concat_axis=0, tiled=True)  10.3 us
    ppermute x2, starting transfers between devices, extended(): before = lax.ppermute(last, axis, up)  8.46 us
    dot_general x17, matrix products, conv_taps(): jnp.dot(window, weights[3 * row_off + col_off], preferred_element_type=jn...  8.17 us
    ppermute x2, waiting for transfers between devices, extended(): after = lax.ppermute(initial, axis, down)  7.71 us
    all_to_all x1, waiting for transfers between devices, shards(): lax.all_to_all(keyres, 'frame', split_axis=2, concat_axis=0, tiled=True)  6.21 us
    sub x1, matrix products, shards(): weights_soft = jax.nn.softmax(scores, axis=-1).astype(jnp.bfloat16)  5.4 us
    unnamed x27, local copies, waits for them, and re-layouts  5.36 us
  transfers between devices with their start and end apart: 6, of which 5 were waited for; matrix products, arithmetic and copies ran while one was open for 3% of the time, Pallas kernels for 0%

commit v1 on v0

v1 whole, which is shorter than its diff:
```python
import functools
import math

import jax
import jax.numpy as jnp
import numpy as np
from jax import lax
from jax.experimental import pallas as pl
from jax.experimental.pallas import tpu as pltpu
from jax.sharding import PartitionSpec as P

HEADS = 8
MESH = pl.DeviceIdType.MESH
F32 = jnp.float32
BF16 = jnp.bfloat16


def positions(frame_total, channels):
    frame_pos = np.arange(frame_total, dtype=np.float64)[:, None]
    half_index = np.arange(channels // 2, dtype=np.float64)
    frequency = np.exp(half_index * (-2.0 * math.log(10000.0) / channels))
    angles = frame_pos * frequency
    stacked = np.stack([np.sin(angles), np.cos(angles)], axis=-1)
    return stacked.reshape(frame_total, channels).astype(np.float32)


def norm(values, gain):
    average = jnp.mean(values, axis=-1, keepdims=True)
    centered = values - average
    variance = jnp.mean(centered * centered, axis=-1, keepdims=True)
    return centered * lax.rsqrt(variance + 1e-05) * gain


def silu(values):
    return values / (1.0 + jnp.exp(-values))


def dot(left, right):
    return jnp.dot(left, right, preferred_element_type=F32)


def conv_local(images, weights, sums):
    count, rows, cols, channels = images.shape
    whole = images[...].reshape(-1, channels)
    for b in range(3):
        sums[b] = dot(whole, weights[3 + b]).reshape(count, rows, cols, channels)
    if rows > 1:
        upper = images[:, : rows - 1].reshape(-1, channels)
        lower = images[:, 1:].reshape(-1, channels)
        part = (count, rows - 1, cols, channels)
        for b in range(3):
            sums[b, :, 1:] += dot(upper, weights[b]).reshape(part)
            sums[b, :, : rows - 1] += dot(lower, weights[6 + b]).reshape(part)


def conv_edge(edge, weights, sums, row, taps):
    count, cols, channels = edge.shape
    flat = edge[...].reshape(-1, channels)
    for b in range(3):
        sums[b, :, row] += dot(flat, weights[taps + b]).reshape(count, cols, channels)


def conv_row(sums, index, row):
    left, middle, right = (sums[b, index, row] for b in range(3))
    cols = middle.shape[0]
    col = lax.broadcasted_iota(jnp.int32, middle.shape, 0)
    left = jnp.where(col == 0, 0.0, pltpu.roll(left, 1, 0))
    right = jnp.where(col == cols - 1, 0.0, pltpu.roll(right, cols - 1, 0))
    return left + middle + right


def kernel(
    n,
    row_total,
    lat,
    cond,
    key_frames,
    propagate,
    encoding,
    gain_a,
    gain_c,
    enc_hbm,
    zero_hbm,
    q_hbm,
    k_hbm,
    v_hbm,
    o_hbm,
    blk_hbm,
    out,
    enc_w,
    zero_w,
    q_w,
    k_w,
    v_w,
    o_w,
    blk_w,
    lat_pix,
    keyres,
    res_pix,
    hidden,
    att_pix,
    att,
    act,
    cond_top,
    cond_bot,
    act_top,
    act_bot,
    sums_e,
    sums_b,
    w_sem,
    own_sem,
    lat_send,
    lat_recv,
    res_send,
    res_recv,
    att_send,
    att_recv,
    ch_send,
    ch_recv,
    ah_send,
    ah_recv,
):
    me = lax.axis_index("frame")
    row_me = lax.axis_index("row")
    frames_dev, _, pix, channels = lat.shape
    slots, rows, cols, _ = cond.shape
    frames = frames_dev * n
    head_dim = channels // HEADS
    has_up = row_me > 0
    has_down = row_me < row_total - 1

    pairs = [
        (enc_hbm, enc_w),
        (zero_hbm, zero_w),
        (q_hbm, q_w),
        (k_hbm, k_w),
        (v_hbm, v_w),
        (o_hbm, o_w),
        (blk_hbm, blk_w),
    ]
    loads = [pltpu.make_async_copy(s, d, w_sem.at[i]) for i, (s, d) in enumerate(pairs)]
    for load in loads:
        load.start()

    barrier = pltpu.get_barrier_semaphore()
    for k in range(1, n):
        pl.semaphore_signal(
            barrier, inc=1, device_id={"frame": lax.rem(me + k, n)}, device_id_type=MESH
        )

    @pl.when(has_up)
    def _():
        pl.semaphore_signal(barrier, inc=1, device_id={"row": row_me - 1}, device_id_type=MESH)

    @pl.when(has_down)
    def _():
        pl.semaphore_signal(barrier, inc=1, device_id={"row": row_me + 1}, device_id_type=MESH)

    neighbours = has_up.astype(jnp.int32) + has_down.astype(jnp.int32)
    pl.semaphore_wait(barrier, n - 1 + neighbours)

    def remote(src, dst, send, recv, **where):
        return pltpu.make_async_remote_copy(
            src_ref=src,
            dst_ref=dst,
            send_sem=send,
            recv_sem=recv,
            device_id=where,
            device_id_type=MESH,
        )

    def up(src, dst, send, recv):
        return remote(src, dst, send, recv, row=row_me - 1)

    def down(src, dst, send, recv):
        return remote(src, dst, send, recv, row=row_me + 1)

    cond_up = up(cond.at[:, 0], cond_bot, ch_send.at[0], ch_recv.at[0])
    cond_down = down(cond.at[:, rows - 1], cond_top, ch_send.at[1], ch_recv.at[1])
    pl.when(has_up)(cond_up.start)
    pl.when(has_down)(cond_down.start)

    def spread(src, dst, count, send, recv):
        copies = []
        for k in range(1, n):
            peer = lax.rem(me + k, n)
            copies.append(
                remote(
                    src.at[:, peer],
                    dst.at[pl.ds(me * count, count)],
                    send.at[k],
                    recv.at[k],
                    frame=peer,
                )
            )
        return copies

    lat_copies = spread(lat, lat_pix, frames_dev, lat_send, lat_recv)
    for copy in lat_copies:
        copy.start()
    lat_own = pltpu.make_async_copy(
        lat.at[:, me], lat_pix.at[pl.ds(me * frames_dev, frames_dev)], own_sem.at[0]
    )
    lat_own.start()

    @pl.when(jnp.logical_not(has_up))
    def _():
        cond_top[...] = jnp.zeros_like(cond_top)
        act_top[...] = jnp.zeros_like(act_top)

    @pl.when(jnp.logical_not(has_down))
    def _():
        cond_bot[...] = jnp.zeros_like(cond_bot)
        act_bot[...] = jnp.zeros_like(act_bot)

    loads[0].wait()
    conv_local(cond, enc_w, sums_e)
    pl.when(has_up)(cond_down.wait_recv)
    pl.when(has_down)(cond_up.wait_recv)
    conv_edge(cond_top, enc_w, sums_e, 0, 0)
    conv_edge(cond_bot, enc_w, sums_e, rows - 1, 6)
    loads[1].wait()
    encoded = jnp.concatenate(
        [silu(conv_row(sums_e, s, r)) for s in range(slots) for r in range(rows)], axis=0
    ).astype(BF16)
    keyres[...] = dot(encoded, zero_w[...]).reshape(keyres.shape).astype(BF16)
    res_copies = spread(keyres, res_pix, slots, res_send, res_recv)
    for copy in res_copies:
        copy.start()
    res_own = pltpu.make_async_copy(
        keyres.at[:, me], res_pix.at[pl.ds(me * slots, slots)], own_sem.at[1]
    )
    res_own.start()

    lat_own.wait()
    for copy in lat_copies:
        copy.wait()
    res_own.wait()
    for copy in res_copies:
        copy.wait()

    def hide(f, carry):
        slot = propagate[f]
        gap = jnp.abs(f - key_frames[slot]).astype(F32)
        reach = jnp.exp(jnp.full((1, channels), -gap / (2 * frames_dev), F32))
        value = lat_pix[f].astype(F32) + reach * res_pix[slot].astype(F32)
        hidden[f] = value.astype(BF16).astype(F32)
        return carry

    lax.fori_loop(0, frames, hide, 0, unroll=frames <= 24)

    for load in loads[2:6]:
        load.wait()

    chunk = 16 if pix % 16 == 0 else 8
    group = 8
    block = frames * group
    lane = lax.broadcasted_iota(jnp.int32, (1, channels), 1)
    same = lax.rem(lax.broadcasted_iota(jnp.int32, (block, block), 0), group) == lax.rem(
        lax.broadcasted_iota(jnp.int32, (block, block), 1), group
    )
    scale = 1.0 / math.sqrt(head_dim)
    encode = encoding[...][:, None, :]
    att_copies = []
    for c in range(pix // chunk):
        here = hidden[:, c * chunk : (c + 1) * chunk]
        normed = (norm(here, gain_a[...][None]) + encode).reshape(-1, channels).astype(BF16)
        full = (frames, chunk, channels)
        query = dot(normed, q_w[...]).reshape(full)
        keyp = dot(normed, k_w[...]).reshape(full)
        valp = dot(normed, v_w[...]).reshape(full)
        mixed_parts = []
        for g in range(chunk // group):
            part = slice(g * group, (g + 1) * group)
            q_g = query[:, part].reshape(block, channels).astype(BF16)
            k_g = keyp[:, part].reshape(block, channels).astype(BF16)
            v_g = valp[:, part].reshape(block, channels).astype(BF16)

            def head(h, total):
                mine = (lane >= h * head_dim) & (lane < (h + 1) * head_dim)
                pick = jnp.where(mine, 1.0, 0.0).astype(BF16)
                scores = lax.dot_general(
                    q_g * pick, k_g, (((1,), (1,)), ((), ())), preferred_element_type=F32
                )
                scores = jnp.where(same, scores * scale, -1e30)
                top = jnp.max(scores, axis=-1, keepdims=True)
                powers = jnp.exp(scores - top)
                probs = (powers / jnp.sum(powers, axis=-1, keepdims=True)).astype(BF16)
                return total + dot(probs, v_g * pick)

            zero = jnp.zeros((block, channels), F32)
            mixed = lax.fori_loop(0, HEADS, head, zero, unroll=frames <= 24)
            mixed_parts.append(mixed.reshape(frames, group, channels))
        mixed = jnp.concatenate(mixed_parts, axis=1) if len(mixed_parts) > 1 else mixed_parts[0]
        projected = dot(mixed.reshape(-1, channels).astype(BF16), o_w[...]).reshape(full)
        att_pix[c] = (here + projected).astype(BF16)
        for k in range(1, n):
            peer = lax.rem(me + k, n)
            copy = remote(
                att_pix.at[c, pl.ds(peer * frames_dev, frames_dev)],
                att.at[:, me, c],
                att_send.at[c, k],
                att_recv.at[c, k],
                frame=peer,
            )
            copy.start()
            att_copies.append(copy)
        own = pltpu.make_async_copy(
            att_pix.at[c, pl.ds(me * frames_dev, frames_dev)], att.at[:, me, c], own_sem.at[2 + c]
        )
        own.start()
        att_copies.append(own)
    for copy in att_copies:
        copy.wait()

    act_ups, act_downs = [], []
    for f in range(frames_dev):
        value = att[f].astype(F32).reshape(rows * cols, channels)
        act[f] = silu(norm(value, gain_c[...])).reshape(rows, cols, channels).astype(BF16)
        act_up = up(act.at[f, 0], act_bot.at[f], ah_send.at[0, f], ah_recv.at[0, f])
        act_down = down(act.at[f, rows - 1], act_top.at[f], ah_send.at[1, f], ah_recv.at[1, f])
        pl.when(has_up)(act_up.start)
        pl.when(has_down)(act_down.start)
        act_ups.append(act_up)
        act_downs.append(act_down)

    loads[6].wait()
    conv_local(act, blk_w, sums_b)
    for f in range(frames_dev):
        pl.when(has_up)(act_downs[f].wait_recv)
        pl.when(has_down)(act_ups[f].wait_recv)
    conv_edge(act_top, blk_w, sums_b, 0, 0)
    conv_edge(act_bot, blk_w, sums_b, rows - 1, 6)
    for f in range(frames_dev):
        convolved = jnp.concatenate([conv_row(sums_b, f, r) for r in range(rows)], axis=0)
        value = att[f].astype(F32).reshape(rows * cols, channels)
        out[f] = (value + convolved).reshape(rows, cols, channels).astype(BF16)

    pl.when(has_up)(cond_up.wait_send)
    pl.when(has_down)(cond_down.wait_send)
    for f in range(frames_dev):
        pl.when(has_up)(act_ups[f].wait_send)
        pl.when(has_down)(act_downs[f].wait_send)


def shards(
    latents,
    condition,
    key_frames,
    propagate,
    encoder_conv,
    zero_conv,
    attention_gain,
    query_weight,
    key_weight,
    value_weight,
    output_weight,
    conv_gain,
    block_conv,
):
    frames_dev, rows, cols, channels = latents.shape
    slots = condition.shape[0]
    n = lax.axis_size("frame")
    row_total = lax.axis_size("row")
    pix = rows * cols // n
    frames = frames_dev * n
    chunk = 16 if pix % 16 == 0 else 8
    chunks = pix // chunk
    encoding = jnp.asarray(positions(frames, channels))
    square = (channels, channels)
    vmem = pl.BlockSpec(memory_space=pltpu.VMEM)
    smem = pl.BlockSpec(memory_space=pltpu.SMEM)
    anywhere = pl.BlockSpec(memory_space=pl.ANY)
    dma = pltpu.SemaphoreType.DMA
    return pl.pallas_call(
        functools.partial(kernel, n, row_total),
        out_shape=jax.ShapeDtypeStruct(latents.shape, BF16),
        in_specs=[vmem, vmem, smem, smem, vmem, vmem, vmem] + [anywhere] * 7,
        out_specs=vmem,
        scratch_shapes=[
            pltpu.VMEM((9,) + square, BF16),
            pltpu.VMEM(square, BF16),
            pltpu.VMEM(square, BF16),
            pltpu.VMEM(square, BF16),
            pltpu.VMEM(square, BF16),
            pltpu.VMEM(square, BF16),
            pltpu.VMEM((9,) + square, BF16),
            pltpu.VMEM((frames, pix, channels), BF16),
            pltpu.VMEM((slots, n, pix, channels), BF16),
            pltpu.VMEM((slots * n, pix, channels), BF16),
            pltpu.VMEM((frames, pix, channels), F32),
            pltpu.VMEM((chunks, frames, chunk, channels), BF16),
            pltpu.VMEM((frames_dev, n, chunks, chunk, channels), BF16),
            pltpu.VMEM((frames_dev, rows, cols, channels), BF16),
            pltpu.VMEM((slots, cols, channels), BF16),
            pltpu.VMEM((slots, cols, channels), BF16),
            pltpu.VMEM((frames_dev, cols, channels), BF16),
            pltpu.VMEM((frames_dev, cols, channels), BF16),
            pltpu.VMEM((3, slots, rows, cols, channels), F32),
            pltpu.VMEM((3, frames_dev, rows, cols, channels), F32),
            dma((7,)),
            dma((2 + chunks,)),
            dma((n,)),
            dma((n,)),
            dma((n,)),
            dma((n,)),
            dma((chunks, n)),
            dma((chunks, n)),
            dma((2,)),
            dma((2,)),
            dma((2, frames_dev)),
            dma((2, frames_dev)),
        ],
        compiler_params=pltpu.CompilerParams(
            collective_id=0, has_side_effects=True, vmem_limit_bytes=60 * 1024 * 1024
        ),
    )(
        latents.reshape(frames_dev, n, pix, channels),
        condition,
        key_frames,
        propagate,
        encoding,
        attention_gain.reshape(1, channels),
        conv_gain.reshape(1, channels),
        encoder_conv,
        zero_conv,
        query_weight,
        key_weight,
        value_weight,
        output_weight,
        block_conv,
    )


def solution(mesh):
    placed = (
        P(("group", "frame"), "row", None, None),
        P(("group", "frame"), "row", None, None),
        P("group"),
        P("group"),
        P(),
        P(),
        P(),
        P(),
        P(),
        P(),
        P(),
        P(),
        P(),
    )
    return jax.shard_map(
        shards,
        mesh=mesh,
        in_specs=placed,
        out_specs=P(("group", "frame"), "row", None, None),
        check_vma=False,
    )
```

time: 120 us -> 50.5 us (0.42)
  Pallas kernels: 0 us -> 45.8 us
  waiting for transfers between devices: 28.6 us -> 0 us
  local copies, waits for them, and re-layouts: 32.3 us -> 4.46 us
  matrix products: 22.9 us -> 0 us
  starting transfers between devices: 18.3 us -> 0 us
  blocking collectives: 11.9 us -> 0 us
  other arithmetic: 4.6 us -> 0 us
    pallas_call x0 -> x1, Pallas kernels: none -> 45.8 us  [shards(): pl.pallas_call(functools.partial(kernel, n, row_total), out_shape=jax.Sha...]
    dot_general x24 -> x0, matrix products: 17.5 us -> none  [the longest x17 8.17 us: conv_taps(): jnp.dot(window, weights[3 * row_off + col_off], preferred_element_type=jn...]
    reshape x10 -> x2, local copies, waits for them, and re-layouts: 19.6 us -> 2.52 us  [the longest x1 1.28 us: shards(): conv_gain.reshape(1, channels)]
    all_to_all x2 -> x0, waiting for transfers between devices: 16.5 us -> none  [the longest x1 10.3 us: shards(): lax.all_to_all(latents, 'frame', split_axis=2, concat_axis=0, tiled=True)]
    ppermute x4 -> x0, waiting for transfers between devices: 12.1 us -> none  [the longest x2 7.71 us: extended(): after = lax.ppermute(initial, axis, down)]
    all_to_all x1 -> x0, blocking collectives: 11.9 us -> none  [shards(): lax.all_to_all(attended_pix, 'frame', split_axis=0, concat_axis=2, tiled=...]
    ppermute x4 -> x0, starting transfers between devices: 11 us -> none  [the longest x2 8.46 us: extended(): before = lax.ppermute(last, axis, up)]
    all_to_all x2 -> x0, starting transfers between devices: 7.26 us -> none  [the longest x1 3.67 us: shards(): lax.all_to_all(latents, 'frame', split_axis=2, concat_axis=0, tiled=True)]
  transfers between devices with their start and end apart: 6 -> 0, of which waited for: 5 -> 0; matrix products, arithmetic and copies ran while one was open for 3% -> 0% of each run, Pallas kernels for 0% -> 0%
where the time goes in v1:
time: 50.5 us; the launch traced here: 50.3 us
  Pallas kernels  45.8 us (91%)
  local copies, waits for them, and re-layouts  4.46 us (9%)
    pallas_call x1, Pallas kernels, shards(): pl.pallas_call(functools.partial(kernel, n, row_total), out_shape=jax.Sha...  45.8 us
    unnamed x1, local copies, waits for them, and re-layouts  1.94 us
    reshape x1, local copies, waits for them, and re-layouts, shards(): conv_gain.reshape(1, channels)  1.28 us
    reshape x1, local copies, waits for them, and re-layouts, shards(): attention_gain.reshape(1, channels)  1.24 us

profile of v1, /device:TPU:0, one launch (start us, length us, event | category | flops | bytes accessed | tf_op | source)
XLA Modules:
  0.0 50.3 jit_solution(8477163816911740225)
XLA Ops:
  0.0 1.2 %reshape.10.gain_a = f32[1,320]{1,0:T(1,128)} reshape(f32[320]{0:T(512)} %param.20) | data formatting | bytes 2560 | tf_op jit(solution)/shard_map/reshape | solution.py:423
  1.2 1.3 %reshape.11.gain_c = f32[1,320]{1,0:T(1,128)} reshape(f32[320]{0:T(512)} %param.25) | data formatting | bytes 2560 | tf_op jit(solution)/shard_map/reshape | solution.py:424
  2.5 45.8 %shard_map.136 = bf16[6,2,64,320]{3,2,1,0:T(8,128)(2,1)} custom-call(bf16[6,4,32,320]{3,2,1,0:T(8,128)(2,1)} %bitcast.1, bf16[3,2,64,320]{3,2,1,0:T(8,128)(2,1)} %cond.1, s32[12]{0:T(128)} %key_frames.1, s32[24]{0:T(128)} %propagate.1, f32[24,320]{1,0:T(8,128)} %constant.2.clone.encoding, f32[1,320]{1,0:T(1,128)} %reshape.10.gain_a, ...), custom_call_target="tpu_custom_call" | custom-call | tf_op jit(solution)/shard_map/pallas_call | solution.py:375
  48.4 1.9 %copy.16 = bf16[6,2,64,320]{3,2,1,0:T(8,128)(2,1)} copy(bf16[6,2,64,320]{3,2,1,0:T(8,128)(2,1)} %shard_map.136) | data formatting | bytes 983040

commit v2 on v1

--- a/solution.py
+++ b/solution.py
@@ -39,14 +39,18 @@
     return jnp.dot(left, right, preferred_element_type=F32)
 
 
+def flat(values):
+    return values.astype(F32).reshape(-1, values.shape[-1]).astype(BF16)
+
+
 def conv_local(images, weights, sums):
-    count, rows, cols, channels = images.shape
-    whole = images[...].reshape(-1, channels)
+    _, count, rows, cols, channels = sums.shape
+    whole = flat(images[...])
     for b in range(3):
         sums[b] = dot(whole, weights[3 + b]).reshape(count, rows, cols, channels)
     if rows > 1:
-        upper = images[:, : rows - 1].reshape(-1, channels)
-        lower = images[:, 1:].reshape(-1, channels)
+        upper = flat(images[:, : rows - 1])
+        lower = flat(images[:, 1:])
         part = (count, rows - 1, cols, channels)
         for b in range(3):
             sums[b, :, 1:] += dot(upper, weights[b]).reshape(part)
@@ -54,10 +58,10 @@
 
 
 def conv_edge(edge, weights, sums, row, taps):
-    count, cols, channels = edge.shape
-    flat = edge[...].reshape(-1, channels)
+    _, count, _, cols, channels = sums.shape
+    values = flat(edge[...])
     for b in range(3):
-        sums[b, :, row] += dot(flat, weights[taps + b]).reshape(count, cols, channels)
+        sums[b, :, row] += dot(values, weights[taps + b]).reshape(count, cols, channels)
 
 
 def conv_row(sums, index, row):
@@ -73,7 +77,7 @@
     n,
     row_total,
     lat,
-    cond,
+    cond_hbm,
     key_frames,
     propagate,
     encoding,
@@ -87,6 +91,7 @@
     o_hbm,
     blk_hbm,
     out,
+    cond,
     enc_w,
     zero_w,
     q_w,
@@ -124,12 +129,17 @@
     row_me = lax.axis_index("row")
     frames_dev, _, pix, channels = lat.shape
     slots, rows, cols, _ = cond.shape
+    chunks = res_recv.shape[0]
+    chunk = pix // chunks
+    group = att.shape[3]
+    per_chunk = chunk // group
     frames = frames_dev * n
     head_dim = channels // HEADS
     has_up = row_me > 0
     has_down = row_me < row_total - 1
 
     pairs = [
+        (cond_hbm, cond),
         (enc_hbm, enc_w),
         (zero_hbm, zero_w),
         (q_hbm, q_w),
@@ -175,8 +185,8 @@
     def down(src, dst, send, recv):
         return remote(src, dst, send, recv, row=row_me + 1)
 
-    cond_up = up(cond.at[:, 0], cond_bot, ch_send.at[0], ch_recv.at[0])
-    cond_down = down(cond.at[:, rows - 1], cond_top, ch_send.at[1], ch_recv.at[1])
+    cond_up = up(cond_hbm.at[:, 0], cond_bot, ch_send.at[0], ch_recv.at[0])
+    cond_down = down(cond_hbm.at[:, rows - 1], cond_top, ch_send.at[1], ch_recv.at[1])
     pl.when(has_up)(cond_up.start)
     pl.when(has_down)(cond_down.start)
 
@@ -214,121 +224,167 @@
         act_bot[...] = jnp.zeros_like(act_bot)
 
     loads[0].wait()
+    loads[1].wait()
     conv_local(cond, enc_w, sums_e)
     pl.when(has_up)(cond_down.wait_recv)
     pl.when(has_down)(cond_up.wait_recv)
     conv_edge(cond_top, enc_w, sums_e, 0, 0)
     conv_edge(cond_bot, enc_w, sums_e, rows - 1, 6)
-    loads[1].wait()
+    loads[2].wait()
     encoded = jnp.concatenate(
         [silu(conv_row(sums_e, s, r)) for s in range(slots) for r in range(rows)], axis=0
     ).astype(BF16)
     keyres[...] = dot(encoded, zero_w[...]).reshape(keyres.shape).astype(BF16)
-    res_copies = spread(keyres, res_pix, slots, res_send, res_recv)
-    for copy in res_copies:
-        copy.start()
-    res_own = pltpu.make_async_copy(
-        keyres.at[:, me], res_pix.at[pl.ds(me * slots, slots)], own_sem.at[1]
-    )
-    res_own.start()
+    res_copies = []
+    for c in range(chunks):
+        span = pl.ds(c * chunk, chunk)
+        for k in range(1, n):
+            peer = lax.rem(me + k, n)
+            copy = remote(
+                keyres.at[:, peer, span],
+                res_pix[c].at[pl.ds(me * slots, slots)],
+                res_send.at[c, k],
+                res_recv.at[c, k],
+                frame=peer,
+            )
+            copy.start()
+            res_copies.append(copy)
+        own = pltpu.make_async_copy(
+            keyres.at[:, me, span], res_pix[c].at[pl.ds(me * slots, slots)], own_sem.at[1 + c]
+        )
+        own.start()
+        res_copies.append(own)
 
     lat_own.wait()
     for copy in lat_copies:
         copy.wait()
-    res_own.wait()
-    for copy in res_copies:
-        copy.wait()
-
-    def hide(f, carry):
-        slot = propagate[f]
-        gap = jnp.abs(f - key_frames[slot]).astype(F32)
-        reach = jnp.exp(jnp.full((1, channels), -gap / (2 * frames_dev), F32))
-        value = lat_pix[f].astype(F32) + reach * res_pix[slot].astype(F32)
-        hidden[f] = value.astype(BF16).astype(F32)
-        return carry
-
-    lax.fori_loop(0, frames, hide, 0, unroll=frames <= 24)
-
-    for load in loads[2:6]:
+
+    for load in loads[3:7]:
         load.wait()
 
-    chunk = 16 if pix % 16 == 0 else 8
-    group = 8
+    small = frames <= 24
     block = frames * group
-    lane = lax.broadcasted_iota(jnp.int32, (1, channels), 1)
     same = lax.rem(lax.broadcasted_iota(jnp.int32, (block, block), 0), group) == lax.rem(
         lax.broadcasted_iota(jnp.int32, (block, block), 1), group
     )
     scale = 1.0 / math.sqrt(head_dim)
     encode = encoding[...][:, None, :]
+
+    def head(h, start, queries, keys, values):
+        lane = start + lax.broadcasted_iota(jnp.int32, (1, queries.shape[1]), 1)
+        mine = (lane >= h * head_dim) & (lane < (h + 1) * head_dim)
+        pick = jnp.where(mine, 1.0, 0.0).astype(BF16)
+        scores = lax.dot_general(
+            queries * pick, keys, (((1,), (1,)), ((), ())), preferred_element_type=F32
+        )
+        scores = jnp.where(same, scores * scale, -1e30)
+        top = jnp.max(scores, axis=-1, keepdims=True)
+        powers = jnp.exp(scores - top)
+        probs = (powers / jnp.sum(powers, axis=-1, keepdims=True)).astype(BF16)
+        return dot(probs, values * pick)
+
+    def windows(h):
+        start = -(-max(0, (h + 1) * head_dim - 256) // 128) * 128
+        return start, min(start + 256, channels)
+
+    def attend(queries, keys, values):
+        if not small or head_dim > 128:
+            return lax.fori_loop(
+                0,
+                HEADS,
+                lambda h, total: total + head(h, 0, queries, keys, values),
+                jnp.zeros((block, channels), F32),
+            )
+        totals = {}
+        for h in range(HEADS):
+            start, stop = windows(h)
+            cut = slice(start, stop)
+            mixed = head(h, start, queries[:, cut], keys[:, cut], values[:, cut])
+            totals[start] = mixed if start not in totals else totals[start] + mixed
+        tiles = []
+        for low in range(0, channels, 128):
+            high = min(low + 128, channels)
+            held = [
+                value[:, low - start : high - start]
+                for start, value in totals.items()
+                if start <= low and high <= start + value.shape[1]
+            ]
+            tiles.append(sum(held[1:], held[0]))
+        return jnp.concatenate(tiles, axis=1)
+
     att_copies = []
-    for c in range(pix // chunk):
-        here = hidden[:, c * chunk : (c + 1) * chunk]
-        normed = (norm(here, gain_a[...][None]) + encode).reshape(-1, channels).astype(BF16)
+    for c in range(chunks):
+        span = slice(c * chunk, (c + 1) * chunk)
+        for copy in res_copies[c * n : (c + 1) * n]:
+            copy.wait()
+
+        def hide(f, carry):
+            slot = propagate[f]
+            gap = jnp.abs(f - key_frames[slot]).astype(F32)
+            reach = jnp.exp(jnp.full((1, channels), -gap / (2 * frames_dev), F32))
+            value = lat_pix[f, span].astype(F32) + reach * res_pix[c][slot].astype(F32)
+            hidden[f, span] = value.astype(BF16).astype(F32)
+            return carry
+
+        lax.fori_loop(0, frames, hide, 0, unroll=small)
+        here = hidden[:, span]
+        normed = (norm(here, gain_a[...]) + encode).reshape(-1, channels).astype(BF16)
         full = (frames, chunk, channels)
         query = dot(normed, q_w[...]).reshape(full)
         keyp = dot(normed, k_w[...]).reshape(full)
         valp = dot(normed, v_w[...]).reshape(full)
-        mixed_parts = []
-        for g in range(chunk // group):
+        for g in range(per_chunk):
+            s = c * per_chunk + g
             part = slice(g * group, (g + 1) * group)
-            q_g = query[:, part].reshape(block, channels).astype(BF16)
-            k_g = keyp[:, part].reshape(block, channels).astype(BF16)
-            v_g = valp[:, part].reshape(block, channels).astype(BF16)
-
-            def head(h, total):
-                mine = (lane >= h * head_dim) & (lane < (h + 1) * head_dim)
-                pick = jnp.where(mine, 1.0, 0.0).astype(BF16)
-                scores = lax.dot_general(
-                    q_g * pick, k_g, (((1,), (1,)), ((), ())), preferred_element_type=F32
+            mixed = attend(
+                query[:, part].reshape(block, channels).astype(BF16),
+                keyp[:, part].reshape(block, channels).astype(BF16),
+                valp[:, part].reshape(block, channels).astype(BF16),
+            )
+            projected = dot(mixed.astype(BF16), o_w[...]).reshape(frames, group, channels)
+            base = hidden[:, s * group : (s + 1) * group]
+            att_pix[s] = (base + projected).astype(BF16)
+            for k in range(1, n):
+                peer = lax.rem(me + k, n)
+                copy = remote(
+                    att_pix.at[s, pl.ds(peer * frames_dev, frames_dev)],
+                    att.at[:, me, s],
+                    att_send.at[s, k],
+                    att_recv.at[s, k],
+                    frame=peer,
                 )
-                scores = jnp.where(same, scores * scale, -1e30)
-                top = jnp.max(scores, axis=-1, keepdims=True)
-                powers = jnp.exp(scores - top)
-                probs = (powers / jnp.sum(powers, axis=-1, keepdims=True)).astype(BF16)
-                return total + dot(probs, v_g * pick)
-
-            zero = jnp.zeros((block, channels), F32)
-            mixed = lax.fori_loop(0, HEADS, head, zero, unroll=frames <= 24)
-            mixed_parts.append(mixed.reshape(frames, group, channels))
-        mixed = jnp.concatenate(mixed_parts, axis=1) if len(mixed_parts) > 1 else mixed_parts[0]
-        projected = dot(mixed.reshape(-1, channels).astype(BF16), o_w[...]).reshape(full)
-        att_pix[c] = (here + projected).astype(BF16)
-        for k in range(1, n):
-            peer = lax.rem(me + k, n)
-            copy = remote(
-                att_pix.at[c, pl.ds(peer * frames_dev, frames_dev)],
-                att.at[:, me, c],
-                att_send.at[c, k],
-                att_recv.at[c, k],
-                frame=peer,
+                copy.start()
+                att_copies.append(copy)
+            own = pltpu.make_async_copy(
+                att_pix.at[s, pl.ds(me * frames_dev, frames_dev)],
+                att.at[:, me, s],
+                own_sem.at[1 + chunks + s],
             )
-            copy.start()
-            att_copies.append(copy)
-        own = pltpu.make_async_copy(
-            att_pix.at[c, pl.ds(me * frames_dev, frames_dev)], att.at[:, me, c], own_sem.at[2 + c]
+            own.start()
+            att_copies.append(own)
+
+    pieces = chunks * per_chunk
+    piece = (frames_dev, rows, n // rows, group, channels)
+    act_ups, act_downs = [], []
+    for s in range(pieces):
+        for copy in att_copies[s * n : (s + 1) * n]:
+            copy.wait()
+        value = att[:, :, s].astype(F32)
+        act[:, :, :, s] = silu(norm(value, gain_c[...])).astype(BF16).reshape(piece)
+        act_up = up(act.at[:, 0, :, s], act_bot.at[:, :, s], ah_send.at[0, s], ah_recv.at[0, s])
+        act_down = down(
+            act.at[:, rows - 1, :, s], act_top.at[:, :, s], ah_send.at[1, s], ah_recv.at[1, s]
         )
-        own.start()
-        att_copies.append(own)
-    for copy in att_copies:
-        copy.wait()
-
-    act_ups, act_downs = [], []
-    for f in range(frames_dev):
-        value = att[f].astype(F32).reshape(rows * cols, channels)
-        act[f] = silu(norm(value, gain_c[...])).reshape(rows, cols, channels).astype(BF16)
-        act_up = up(act.at[f, 0], act_bot.at[f], ah_send.at[0, f], ah_recv.at[0, f])
-        act_down = down(act.at[f, rows - 1], act_top.at[f], ah_send.at[1, f], ah_recv.at[1, f])
         pl.when(has_up)(act_up.start)
         pl.when(has_down)(act_down.start)
         act_ups.append(act_up)
         act_downs.append(act_down)
 
-    loads[6].wait()
+    loads[7].wait()
     conv_local(act, blk_w, sums_b)
-    for f in range(frames_dev):
-        pl.when(has_up)(act_downs[f].wait_recv)
-        pl.when(has_down)(act_ups[f].wait_recv)
+    for s in range(pieces):
+        pl.when(has_up)(act_downs[s].wait_recv)
+        pl.when(has_down)(act_ups[s].wait_recv)
     conv_edge(act_top, blk_w, sums_b, 0, 0)
     conv_edge(act_bot, blk_w, sums_b, rows - 1, 6)
     for f in range(frames_dev):
@@ -338,9 +394,9 @@
 
     pl.when(has_up)(cond_up.wait_send)
     pl.when(has_down)(cond_down.wait_send)
-    for f in range(frames_dev):
-        pl.when(has_up)(act_ups[f].wait_send)
-        pl.when(has_down)(act_downs[f].wait_send)
+    for s in range(pieces):
+        pl.when(has_up)(act_ups[s].wait_send)
+        pl.when(has_down)(act_downs[s].wait_send)
 
 
 def shards(
@@ -366,6 +422,9 @@
     frames = frames_dev * n
     chunk = 16 if pix % 16 == 0 else 8
     chunks = pix // chunk
+    group = 8
+    pieces = pix // group
+    per_row = n // rows
     encoding = jnp.asarray(positions(frames, channels))
     square = (channels, channels)
     vmem = pl.BlockSpec(memory_space=pltpu.VMEM)
@@ -375,9 +434,10 @@
     return pl.pallas_call(
         functools.partial(kernel, n, row_total),
         out_shape=jax.ShapeDtypeStruct(latents.shape, BF16),
-        in_specs=[vmem, vmem, smem, smem, vmem, vmem, vmem] + [anywhere] * 7,
+        in_specs=[anywhere, anywhere, smem, smem, vmem, vmem, vmem] + [anywhere] * 7,
         out_specs=vmem,
         scratch_shapes=[
+            pltpu.VMEM(condition.shape, BF16),
             pltpu.VMEM((9,) + square, BF16),
             pltpu.VMEM(square, BF16),
             pltpu.VMEM(square, BF16),
@@ -387,29 +447,29 @@
             pltpu.VMEM((9,) + square, BF16),
             pltpu.VMEM((frames, pix, channels), BF16),
             pltpu.VMEM((slots, n, pix, channels), BF16),
-            pltpu.VMEM((slots * n, pix, channels), BF16),
+            [pltpu.VMEM((slots * n, chunk, channels), BF16) for _ in range(chunks)],
             pltpu.VMEM((frames, pix, channels), F32),
-            pltpu.VMEM((chunks, frames, chunk, channels), BF16),
-            pltpu.VMEM((frames_dev, n, chunks, chunk, channels), BF16),
-            pltpu.VMEM((frames_dev, rows, cols, channels), BF16),
+            pltpu.VMEM((pieces, frames, group, channels), BF16),
+            pltpu.VMEM((frames_dev, n, pieces, group, channels), BF16),
+            pltpu.VMEM((frames_dev, rows, per_row, pieces, group, channels), BF16),
             pltpu.VMEM((slots, cols, channels), BF16),
             pltpu.VMEM((slots, cols, channels), BF16),
-            pltpu.VMEM((frames_dev, cols, channels), BF16),
-            pltpu.VMEM((frames_dev, cols, channels), BF16),
+            pltpu.VMEM((frames_dev, per_row, pieces, group, channels), BF16),
+            pltpu.VMEM((frames_dev, per_row, pieces, group, channels), BF16),
             pltpu.VMEM((3, slots, rows, cols, channels), F32),
             pltpu.VMEM((3, frames_dev, rows, cols, channels), F32),
-            dma((7,)),
-            dma((2 + chunks,)),
-            dma((n,)),
-            dma((n,)),
+            dma((8,)),
+            dma((1 + chunks + pieces,)),
             dma((n,)),
             dma((n,)),
             dma((chunks, n)),
             dma((chunks, n)),
+            dma((pieces, n)),
+            dma((pieces, n)),
             dma((2,)),
             dma((2,)),
-            dma((2, frames_dev)),
-            dma((2, frames_dev)),
+            dma((2, pieces)),
+            dma((2, pieces)),
         ],
         compiler_params=pltpu.CompilerParams(
             collective_id=0, has_side_effects=True, vmem_limit_bytes=60 * 1024 * 1024
@@ -420,8 +480,8 @@
         key_frames,
         propagate,
         encoding,
-        attention_gain.reshape(1, channels),
-        conv_gain.reshape(1, channels),
+        attention_gain,
+        conv_gain,
         encoder_conv,
         zero_conv,
         query_weight,

time: 50.5 us -> 36.2 us (0.72)
  Pallas kernels: 45.8 us -> 34 us
  local copies, waits for them, and re-layouts: 4.46 us -> 1.94 us
    pallas_call x1, Pallas kernels: 45.8 us -> 34 us  [shards(): pl.pallas_call(functools.partial(kernel, n, row_total), out_shape=jax.Sha...]
    reshape x2 -> x0, local copies, waits for them, and re-layouts: 2.52 us -> none  [the longest x1 1.28 us: shards(): conv_gain.reshape(1, channels)]
where the time goes in v2:
time: 36.2 us; the launch traced here: 36 us
  Pallas kernels  34 us (94%)
  local copies, waits for them, and re-layouts  1.94 us (5%)
    pallas_call x1, Pallas kernels, shards(): pl.pallas_call(functools.partial(kernel, n, row_total), out_shape=jax.Sha...  34 us
    unnamed x1, local copies, waits for them, and re-layouts  1.94 us

profile of v2, /device:TPU:0, one launch (start us, length us, event | category | flops | bytes accessed | tf_op | source)
XLA Modules:
  0.0 36.0 jit_solution(15250585871397030682)
XLA Ops:
  0.0 34.0 %shard_map.136 = bf16[6,2,64,320]{3,2,1,0:T(8,128)(2,1)} custom-call(bf16[6,4,32,320]{3,2,1,0:T(8,128)(2,1)} %bitcast.1, bf16[3,2,64,320]{3,2,1,0:T(8,128)(2,1)} %cond_hbm.1, s32[12]{0:T(128)} %key_frames.1, s32[24]{0:T(128)} %propagate.1, f32[24,320]{1,0:T(8,128)} %constant.2.clone.encoding, f32[320]{0:T(512)} %gain_a.1, f32[320]{0:T(512)} %gain_c.1, ...), custom_call_target="tpu_custom_call" | custom-call | tf_op jit(solution)/shard_map/pallas_call | solution.py:434
  34.0 1.9 %copy.16 = bf16[6,2,64,320]{3,2,1,0:T(8,128)(2,1)} copy(bf16[6,2,64,320]{3,2,1,0:T(8,128)(2,1)} %shard_map.136) | data formatting | bytes 983040
